TPU v7x, 32 devices: a whole 2x2x4 slice. The times are simulated.
32 devices in a mesh: ctx: 16 (over z, y, x), tp: 2 (over core).
Axes of the slice: x: 2, y: 2, z: 4, core: 2. Of those that a mesh axis runs over, the one named last changes fastest.
Arguments:
- hidden_states: bfloat16 [4096, 8192], P('ctx', 'tp'), may hold values from -6 to 6
- queries: bfloat16 [4096, 4096], P('ctx', 'tp')
- key_matrix: bfloat16 [8192, 1024], P('tp'), may hold values from -0.0625 to 0.0625
- value_matrix: bfloat16 [8192, 1024], P('tp'), may hold values from -0.0625 to 0.0625
- stretch_table: int32 [32], replicated, may hold values from 0 to 31, as said below
Outputs:
- attended: bfloat16 [4096, 4096], P('ctx', 'tp')
Inputs may be any that keep to these rules, and one draw needn't show every extreme that they name: `stretch_table`: a permutation of 0 to 31 in which entries 2 i and 2 i + 1 are two stretches c and 31 - c.
All inputs are finite; a program needn't handle non-finite values.
Results may differ from a plain program's by a relative error of at most 0.007.
The roundings to bfloat16 on the way count: a program that leaves them out, or rounds other values in their place, can miss the bound.
Values may be sent and summed in bfloat16 or wider, within the bound.
A program may use at most 256 MiB of HBM per device.

v0:
```python
import math
import jax
import jax.numpy as jnp
from jax import lax
from jax.sharding import PartitionSpec as P

KEY_VALUE_HEADS = 8
HEAD_SIZE = 128


def stretch_position(stretch_ids, stretch_table):
    listed = jnp.arange(stretch_table.shape[0], dtype=jnp.int32)
    onehot = stretch_ids[:, None] == listed[None, :]
    return jnp.sum(jnp.where(onehot, stretch_table[None, :], 0), axis=1)


def body(hidden_states, queries, key_matrix, value_matrix, stretch_table):
    tokens_dev = hidden_states.shape[0]
    key_tiles = key_matrix.reshape(key_matrix.shape[0], KEY_VALUE_HEADS, HEAD_SIZE)
    value_tiles = value_matrix.reshape(value_matrix.shape[0], KEY_VALUE_HEADS, HEAD_SIZE)
    head_group = KEY_VALUE_HEADS // lax.axis_size("tp")
    key_term = jnp.einsum(
        "tc,chd->htd", hidden_states, key_tiles, preferred_element_type=jnp.float32
    )
    value_term = jnp.einsum(
        "tc,chd->htd", hidden_states, value_tiles, preferred_element_type=jnp.float32
    )
    shares = lax.psum_scatter(
        jnp.stack([key_term, value_term], axis=1), "tp", scatter_dimension=0, tiled=True
    )
    kv_local = shares.astype(jnp.bfloat16).transpose(2, 0, 1, 3)
    stretch = tokens_dev // 2
    ctx_size = lax.axis_size("ctx")
    all_rows = jnp.arange(ctx_size * tokens_dev, dtype=jnp.int32)
    all_places = stretch_position(all_rows // stretch, stretch_table) * stretch + all_rows % stretch
    device = lax.axis_index("ctx")
    query_place = lax.dynamic_slice_in_dim(all_places, device * tokens_dev, tokens_dev, 0)
    query_heads = queries.shape[1] // HEAD_SIZE
    group_ratio = query_heads // head_group
    query_grid = queries.reshape(tokens_dev, head_group, group_ratio, HEAD_SIZE)
    scale = 1.0 / HEAD_SIZE**0.5
    span_queries = (query_grid[:stretch], query_grid[stretch:])
    span_places = (query_place[:stretch], query_place[stretch:])
    span_latest = (jnp.max(span_places[0]), jnp.max(span_places[1]))

    def fresh():
        return (
            jnp.full((head_group, group_ratio, stretch), -1e30, jnp.float32),
            jnp.zeros((head_group, group_ratio, stretch), jnp.float32),
            jnp.zeros((head_group, group_ratio, stretch, HEAD_SIZE), jnp.float32),
        )

    carry = (fresh(), fresh())
    piece = lax.all_gather(kv_local, "ctx", axis=0, tiled=True)
    rows = piece.shape[0]
    width = math.gcd(rows, 1024)
    blocks = rows // width

    def visit(state, index):
        begin = index * width
        block = lax.dynamic_slice_in_dim(piece, begin, width, 0)
        key_place = lax.dynamic_slice_in_dim(all_places, begin, width, 0)
        earliest = jnp.min(key_place)
        key_block = block[:, :, 0]
        value_block = block[:, :, 1]
        updated = []
        for span in range(2):
            span_grid = span_queries[span]
            places = span_places[span]

            def attend(inner, span_grid=span_grid, places=places):
                highs, sums, partial_value = inner
                score = (
                    jnp.einsum(
                        "tgrd,ngd->grtn", span_grid, key_block, preferred_element_type=jnp.float32
                    )
                    * scale
                )
                visible = key_place[None, :] <= places[:, None]
                masked = jnp.where(visible, score, jnp.float32(-1e30))
                new_high = jnp.maximum(highs, jnp.max(masked, axis=-1))
                weight = jnp.where(visible, jnp.exp(masked - new_high[..., None]), jnp.float32(0.0))
                factor = jnp.exp(highs - new_high)
                sums = sums * factor + jnp.sum(weight, axis=-1)
                update = jnp.einsum(
                    "grtn,ngd->grtd",
                    weight.astype(jnp.bfloat16),
                    value_block,
                    preferred_element_type=jnp.float32,
                )
                partial_value = partial_value * factor[..., None] + update
                return (new_high, sums, partial_value)

            def keep_state(inner):
                return inner

            updated.append(lax.cond(earliest <= span_latest[span], attend, keep_state, state[span]))
        return ((updated[0], updated[1]), None)

    carry, _ = lax.scan(visit, carry, jnp.arange(blocks, dtype=jnp.int32))
    output = jnp.concatenate(
        [carry[0][2] / carry[0][1][..., None], carry[1][2] / carry[1][1][..., None]], axis=2
    )
    return (
        output.transpose(2, 0, 1, 3)
        .reshape(tokens_dev, query_heads * HEAD_SIZE)
        .astype(jnp.bfloat16)
    )


def solution(mesh):
    in_specs = (P("ctx", "tp"), P("ctx", "tp"), P("tp", None), P("tp", None), P())
    out_specs = P("ctx", "tp")
    return jax.shard_map(body, mesh=mesh, in_specs=in_specs, out_specs=out_specs, check_vma=False)
```

profile of v0, /device:TPU:5, one launch (start us, length us, event | category | flops | bytes accessed | tf_op | source)
XLA Modules:
  0.0 292.8 jit_solution(8657823326039178736)
XLA Ops:
  6.5 11.7 %copy.48 = bf16[4096,1024]{0,1:T(8,128)(2,1)} copy(bf16[4096,1024]{1,0:T(8,128)(2,1)} %param.13) | data formatting | bytes 16777216 | tf_op jit(solution)/shard_map/reshape | solution.py:19
  18.2 11.3 %copy.49 = bf16[4096,1024]{0,1:T(8,128)(2,1)} copy(bf16[4096,1024]{1,0:T(8,128)(2,1)} %param.14) | data formatting | bytes 16777216 | tf_op jit(solution)/shard_map/reshape | solution.py:20
  29.6 5.9 %fusion.34 = f32[8,1,256,128]{2,3,0,1:T(8,128)S(1)} fusion(bf16[4096,8,128]{0,2,1:T(8,128)(2,1)} %bitcast.116, bf16[256,4096]{1,0:T(8,128)(2,1)S(1)} %copy-done), kind=kOutput, calls=%fused_computation.41 | convolution fusion | flops 2147483648 | bytes 11534336 | tf_op jit(solution)/shard_map/tc,chd->htd/dot_general | solution.py:22
  35.5 2.4 fusion.37
  38.1 9.5 %all-reduce.2 = bf16[8,2,256,128]{2,3,0,1:T(8,128)(2,1)S(1)} all-reduce(f32[8,2,256,128]{2,3,0,1:T(8,128)S(1)} %pad_maximum_fusion), channel_id=2, replica_groups=mesh['ctx'=16,'tp'=2] {'tp'}, use_global_device_ids=true, to_apply=%region_0.0.clone | all-reduce | flops 524288 | bytes 3145728
  49.7 1.3 fusion.50
  54.5 130.6 %all-gather.2.cloned.1.call-done = bf16[4096,4,2,128]{0,3,1,2:T(8,128)(2,1)} async-done(((bf16[256,4,2,128]{0,3,1,2:T(8,128)(2,1)}), bf16[4096,4,2,128]{0,3,1,2:T(8,128)(2,1)}) %all-gather.2.cloned.1.call-update) | async-done | bytes 8388624 | tf_op jit(solution)/shard_map/all_gather | solution.py:54
  185.1 1.1 broadcast.66.clone
  186.2 1.1 broadcast.66
  187.3 94.1 %while.20 = (s32[]{:T(128)}, f32[4,4,128]{2,1,0:T(4,128)S(1)}, f32[4,4,128]{2,1,0:T(4,128)S(1)}, f32[4,4,128,128]{3,2,1,0:T(8,128)}, f32[4,4,128]{2,1,0:T(4,128)...) while((s32[]{:T(128)}, f32[4,4,128]{2,1,0:T(4,128)S(1)}, ...), condition=%wide.region_14.15_spmd, body=%wide.region_4.14_spmd.sunk | while | flops 2203329536 | bytes 88360624 | solution.py:100
  191.5 1.8 constant_dynamic-slice_fusion.3
  194.6 8.7 %conditional.4 = ((f32[4,4,128]{2,1,0:T(4,128)S(1)}, f32[4,4,128]{2,1,0:T(4,128)S(1)}, f32[4,4,128,128]{3,2,1,0:T(8,128)})) conditional(s32[]{:T(128)} %convert_element_type.38, (f32[4,4,128]{2,1,0:T(4,128)S(1)}, f32[4,4,128]{2,1,0:T(4,128)S(1)}, f32[4,4,128,128]{3,2,1,0:T(8,128)}) %tuple.57, (s32[1024]{0:T(1024)S(1)}, s32[128]{0:T(128)S(1)}, ...), branch_computations={%region_6.6_spmd, %region_7.9_spmd} | conditional | flops 1101664256 | bytes 38933080 | solution.py:97
  194.9 2.5 fusion
  197.3 2.0 fusion.2
  199.4 2.9 %fusion.6 = f32[4,4,128,128]{3,2,1,0:T(8,128)S(1)} fusion(f32[4,1024,128,4]{2,1,3,0:T(8,128)S(1)} %get-tuple-element.265, f32[4,4,128]{2,1,0:T(4,128)S(1)} %max.4, pred[128,1024]{0,1:T(8,128)(4,1)S(1)} %broadcast_compare_fusion, bf16[1024,4,128]{2,0,1:T(8,128)(2,1)S(1)} %get-tuple-element.120, f32[4,4,128,128]{3,2,1,0:T(8,128)S(1)} %copy-done.5, ...), kind=kOutput, calls=%fused_computation.7 | convolution fusion | flops 547880960 | bytes 11681792 | tf_op jit(solution)/shard_map/while/body/eval_jaxpr/cond/branch_1_fun/grtn,ngd->grtd/dot_general | solution.py:85
  203.3 7.6 %conditional.5 = ((f32[4,4,128]{2,1,0:T(4,128)S(1)}, f32[4,4,128]{2,1,0:T(4,128)S(1)}, f32[4,4,128,128]{3,2,1,0:T(8,128)})) conditional(s32[]{:T(128)} %convert_element_type.39, (f32[4,4,128]{2,1,0:T(4,128)S(1)}, f32[4,4,128]{2,1,0:T(4,128)S(1)}, f32[4,4,128,128]{3,2,1,0:T(8,128)}) %tuple.59, (s32[1024]{0:T(1024)S(1)}, s32[128]{0:T(128)S(1)}, ...), branch_computations={%region_10.10_spmd, %region_11.13_spmd} | conditional | flops 1101664256 | bytes 38933080 | solution.py:97
  203.5 1.3 fusion.15
  204.8 2.0 fusion.17
  206.9 2.9 %fusion.21 = f32[4,4,128,128]{3,2,1,0:T(8,128)S(1)} fusion(f32[4,1024,128,4]{2,1,3,0:T(8,128)S(1)} %get-tuple-element.267, f32[4,4,128]{2,1,0:T(4,128)S(1)} %max.5, pred[128,1024]{0,1:T(8,128)(4,1)S(1)} %broadcast_compare_fusion.1, bf16[1024,4,128]{2,0,1:T(8,128)(2,1)S(1)} %get-tuple-element.128, f32[4,4,128,128]{3,2,1,0:T(8,128)S(1)} %copy-done.3, ...), kind=kOutput, calls=%fused_computation.24 | convolution fusion | flops 547880960 | bytes 11681792 | tf_op jit(solution)/shard_map/while/body/eval_jaxpr/cond/branch_1_fun/grtn,ngd->grtd/dot_general | solution.py:85
  215.0 1.8 constant_dynamic-slice_fusion.3
  218.1 8.7 %conditional.4 = ((f32[4,4,128]{2,1,0:T(4,128)S(1)}, f32[4,4,128]{2,1,0:T(4,128)S(1)}, f32[4,4,128,128]{3,2,1,0:T(8,128)})) conditional(s32[]{:T(128)} %convert_element_type.38, (f32[4,4,128]{2,1,0:T(4,128)S(1)}, f32[4,4,128]{2,1,0:T(4,128)S(1)}, f32[4,4,128,128]{3,2,1,0:T(8,128)}) %tuple.57, (s32[1024]{0:T(1024)S(1)}, s32[128]{0:T(128)S(1)}, ...), branch_computations={%region_6.6_spmd, %region_7.9_spmd} | conditional | flops 1101664256 | bytes 38933080 | solution.py:97
  218.4 2.5 fusion
  220.9 2.0 fusion.2
  222.9 2.9 %fusion.6 = f32[4,4,128,128]{3,2,1,0:T(8,128)S(1)} fusion(f32[4,1024,128,4]{2,1,3,0:T(8,128)S(1)} %get-tuple-element.265, f32[4,4,128]{2,1,0:T(4,128)S(1)} %max.4, pred[128,1024]{0,1:T(8,128)(4,1)S(1)} %broadcast_compare_fusion, bf16[1024,4,128]{2,0,1:T(8,128)(2,1)S(1)} %get-tuple-element.120, f32[4,4,128,128]{3,2,1,0:T(8,128)S(1)} %copy-done.5, ...), kind=kOutput, calls=%fused_computation.7 | convolution fusion | flops 547880960 | bytes 11681792 | tf_op jit(solution)/shard_map/while/body/eval_jaxpr/cond/branch_1_fun/grtn,ngd->grtd/dot_general | solution.py:85
  226.8 7.6 %conditional.5 = ((f32[4,4,128]{2,1,0:T(4,128)S(1)}, f32[4,4,128]{2,1,0:T(4,128)S(1)}, f32[4,4,128,128]{3,2,1,0:T(8,128)})) conditional(s32[]{:T(128)} %convert_element_type.39, (f32[4,4,128]{2,1,0:T(4,128)S(1)}, f32[4,4,128]{2,1,0:T(4,128)S(1)}, f32[4,4,128,128]{3,2,1,0:T(8,128)}) %tuple.59, (s32[1024]{0:T(1024)S(1)}, s32[128]{0:T(128)S(1)}, ...), branch_computations={%region_10.10_spmd, %region_11.13_spmd} | conditional | flops 1101664256 | bytes 38933080 | solution.py:97
  227.0 1.3 fusion.15
  228.4 2.0 fusion.17
  230.4 2.9 %fusion.21 = f32[4,4,128,128]{3,2,1,0:T(8,128)S(1)} fusion(f32[4,1024,128,4]{2,1,3,0:T(8,128)S(1)} %get-tuple-element.267, f32[4,4,128]{2,1,0:T(4,128)S(1)} %max.5, pred[128,1024]{0,1:T(8,128)(4,1)S(1)} %broadcast_compare_fusion.1, bf16[1024,4,128]{2,0,1:T(8,128)(2,1)S(1)} %get-tuple-element.128, f32[4,4,128,128]{3,2,1,0:T(8,128)S(1)} %copy-done.3, ...), kind=kOutput, calls=%fused_computation.24 | convolution fusion | flops 547880960 | bytes 11681792 | tf_op jit(solution)/shard_map/while/body/eval_jaxpr/cond/branch_1_fun/grtn,ngd->grtd/dot_general | solution.py:85
  238.5 1.8 constant_dynamic-slice_fusion.3
  241.7 8.7 %conditional.4 = ((f32[4,4,128]{2,1,0:T(4,128)S(1)}, f32[4,4,128]{2,1,0:T(4,128)S(1)}, f32[4,4,128,128]{3,2,1,0:T(8,128)})) conditional(s32[]{:T(128)} %convert_element_type.38, (f32[4,4,128]{2,1,0:T(4,128)S(1)}, f32[4,4,128]{2,1,0:T(4,128)S(1)}, f32[4,4,128,128]{3,2,1,0:T(8,128)}) %tuple.57, (s32[1024]{0:T(1024)S(1)}, s32[128]{0:T(128)S(1)}, ...), branch_computations={%region_6.6_spmd, %region_7.9_spmd} | conditional | flops 1101664256 | bytes 38933080 | solution.py:97
  241.9 2.5 fusion
  244.4 2.0 fusion.2
  246.4 2.9 %fusion.6 = f32[4,4,128,128]{3,2,1,0:T(8,128)S(1)} fusion(f32[4,1024,128,4]{2,1,3,0:T(8,128)S(1)} %get-tuple-element.265, f32[4,4,128]{2,1,0:T(4,128)S(1)} %max.4, pred[128,1024]{0,1:T(8,128)(4,1)S(1)} %broadcast_compare_fusion, bf16[1024,4,128]{2,0,1:T(8,128)(2,1)S(1)} %get-tuple-element.120, f32[4,4,128,128]{3,2,1,0:T(8,128)S(1)} %copy-done.5, ...), kind=kOutput, calls=%fused_computation.7 | convolution fusion | flops 547880960 | bytes 11681792 | tf_op jit(solution)/shard_map/while/body/eval_jaxpr/cond/branch_1_fun/grtn,ngd->grtd/dot_general | solution.py:85
  250.3 7.6 %conditional.5 = ((f32[4,4,128]{2,1,0:T(4,128)S(1)}, f32[4,4,128]{2,1,0:T(4,128)S(1)}, f32[4,4,128,128]{3,2,1,0:T(8,128)})) conditional(s32[]{:T(128)} %convert_element_type.39, (f32[4,4,128]{2,1,0:T(4,128)S(1)}, f32[4,4,128]{2,1,0:T(4,128)S(1)}, f32[4,4,128,128]{3,2,1,0:T(8,128)}) %tuple.59, (s32[1024]{0:T(1024)S(1)}, s32[128]{0:T(128)S(1)}, ...), branch_computations={%region_10.10_spmd, %region_11.13_spmd} | conditional | flops 1101664256 | bytes 38933080 | solution.py:97
  250.6 1.3 fusion.15
  251.9 2.0 fusion.17
  253.9 2.9 %fusion.21 = f32[4,4,128,128]{3,2,1,0:T(8,128)S(1)} fusion(f32[4,1024,128,4]{2,1,3,0:T(8,128)S(1)} %get-tuple-element.267, f32[4,4,128]{2,1,0:T(4,128)S(1)} %max.5, pred[128,1024]{0,1:T(8,128)(4,1)S(1)} %broadcast_compare_fusion.1, bf16[1024,4,128]{2,0,1:T(8,128)(2,1)S(1)} %get-tuple-element.128, f32[4,4,128,128]{3,2,1,0:T(8,128)S(1)} %copy-done.3, ...), kind=kOutput, calls=%fused_computation.24 | convolution fusion | flops 547880960 | bytes 11681792 | tf_op jit(solution)/shard_map/while/body/eval_jaxpr/cond/branch_1_fun/grtn,ngd->grtd/dot_general | solution.py:85
  262.0 1.8 constant_dynamic-slice_fusion.3
  265.2 8.7 %conditional.4 = ((f32[4,4,128]{2,1,0:T(4,128)S(1)}, f32[4,4,128]{2,1,0:T(4,128)S(1)}, f32[4,4,128,128]{3,2,1,0:T(8,128)})) conditional(s32[]{:T(128)} %convert_element_type.38, (f32[4,4,128]{2,1,0:T(4,128)S(1)}, f32[4,4,128]{2,1,0:T(4,128)S(1)}, f32[4,4,128,128]{3,2,1,0:T(8,128)}) %tuple.57, (s32[1024]{0:T(1024)S(1)}, s32[128]{0:T(128)S(1)}, ...), branch_computations={%region_6.6_spmd, %region_7.9_spmd} | conditional | flops 1101664256 | bytes 38933080 | solution.py:97
  265.4 2.5 fusion
  267.9 2.0 fusion.2
  269.9 2.9 %fusion.6 = f32[4,4,128,128]{3,2,1,0:T(8,128)S(1)} fusion(f32[4,1024,128,4]{2,1,3,0:T(8,128)S(1)} %get-tuple-element.265, f32[4,4,128]{2,1,0:T(4,128)S(1)} %max.4, pred[128,1024]{0,1:T(8,128)(4,1)S(1)} %broadcast_compare_fusion, bf16[1024,4,128]{2,0,1:T(8,128)(2,1)S(1)} %get-tuple-element.120, f32[4,4,128,128]{3,2,1,0:T(8,128)S(1)} %copy-done.5, ...), kind=kOutput, calls=%fused_computation.7 | convolution fusion | flops 547880960 | bytes 11681792 | tf_op jit(solution)/shard_map/while/body/eval_jaxpr/cond/branch_1_fun/grtn,ngd->grtd/dot_general | solution.py:85
  273.9 7.6 %conditional.5 = ((f32[4,4,128]{2,1,0:T(4,128)S(1)}, f32[4,4,128]{2,1,0:T(4,128)S(1)}, f32[4,4,128,128]{3,2,1,0:T(8,128)})) conditional(s32[]{:T(128)} %convert_element_type.39, (f32[4,4,128]{2,1,0:T(4,128)S(1)}, f32[4,4,128]{2,1,0:T(4,128)S(1)}, f32[4,4,128,128]{3,2,1,0:T(8,128)}) %tuple.59, (s32[1024]{0:T(1024)S(1)}, s32[128]{0:T(128)S(1)}, ...), branch_computations={%region_10.10_spmd, %region_11.13_spmd} | conditional | flops 1101664256 | bytes 38933080 | solution.py:97
  274.1 1.3 fusion.15
  275.4 2.0 fusion.17
  277.4 2.9 %fusion.21 = f32[4,4,128,128]{3,2,1,0:T(8,128)S(1)} fusion(f32[4,1024,128,4]{2,1,3,0:T(8,128)S(1)} %get-tuple-element.267, f32[4,4,128]{2,1,0:T(4,128)S(1)} %max.5, pred[128,1024]{0,1:T(8,128)(4,1)S(1)} %broadcast_compare_fusion.1, bf16[1024,4,128]{2,0,1:T(8,128)(2,1)S(1)} %get-tuple-element.128, f32[4,4,128,128]{3,2,1,0:T(8,128)S(1)} %copy-done.3, ...), kind=kOutput, calls=%fused_computation.24 | convolution fusion | flops 547880960 | bytes 11681792 | tf_op jit(solution)/shard_map/while/body/eval_jaxpr/cond/branch_1_fun/grtn,ngd->grtd/dot_general | solution.py:85
  281.4 2.1 divide_convert_fusion
  284.4 1.6 convert_element_type.24
  (122 shorter events, 25.9 us)
Async XLA Ops:
  6.5 23.0 %copy-start = (bf16[256,4096]{1,0:T(8,128)(2,1)S(1)}, bf16[256,4096]{1,0:T(8,128)(2,1)}, u32[]{:S(2)}) copy-start(bf16[256,4096]{1,0:T(8,128)(2,1)} %param.11) | copy-start | bytes 6291460
  6.5 178.5 %all-gather.2.cloned.1.call-start = ((), (), s32[]{:S(2)}) async-start(), calls=%async_computation | async-start | bytes 8912896 | tf_op jit(solution)/shard_map/all_gather | solution.py:54
  29.5 5.9 %slice-start = ((s8[8388608]{0:T(1024)(128)(4,1)}), s8[4194304]{0:T(1024)(128)(4,1)S(1)}, s32[]{:S(2)}) async-start(s8[8388608]{0:T(1024)(128)(4,1)} %bitcast.113), calls=%async_computation.1 | async-start | bytes 8388608
  29.5 5.9 %slice-start.1 = ((s8[8388608]{0:T(1024)(128)(4,1)}), s8[4194304]{0:T(1024)(128)(4,1)S(1)}, s32[]{:S(2)}) async-start(s8[8388608]{0:T(1024)(128)(4,1)} %bitcast.113), calls=%async_computation.2 | async-start | bytes 8388608
  35.5 12.1 %copy-start.8 = (u32[32]{0:T(128)S(1)}, u32[32]{0:T(128)}, u32[]{:S(2)}) copy-start(u32[32]{0:T(128)} %constant.81) | copy-start | bytes 388
  37.9 15.7 %copy-start.7 = (s32[32]{0:T(128)S(1)}, s32[32]{0:T(128)}, u32[]{:S(2)}) copy-start(s32[32]{0:T(128)} %param.15) | copy-start | bytes 388
  194.6 8.7 %copy-start.2 = (bf16[128,4,4,128]{3,0,2,1:T(8,128)(2,1)S(1)}, bf16[128,4,4,128]{3,0,2,1:T(8,128)(2,1)}, u32[]{:S(2)}) copy-start(bf16[128,4,4,128]{3,0,2,1:T(8,128)(2,1)} %get-tuple-element.466) | copy-start | bytes 1572868 | tf_op jit(solution)/shard_map/while
  194.9 4.5 %copy-start.5 = (f32[4,4,128,128]{3,2,1,0:T(8,128)S(1)}, f32[4,4,128,128]{3,2,1,0:T(8,128)}, u32[]{:S(2)}) copy-start(f32[4,4,128,128]{3,2,1,0:T(8,128)} %get-tuple-element.119) | copy-start | bytes 3145732 | tf_op jit(solution)/shard_map/while/body/eval_jaxpr/cond
  202.3 1.0 copy-start.6
  203.5 3.4 %copy-start.3 = (f32[4,4,128,128]{3,2,1,0:T(8,128)S(1)}, f32[4,4,128,128]{3,2,1,0:T(8,128)}, u32[]{:S(2)}) copy-start(f32[4,4,128,128]{3,2,1,0:T(8,128)} %get-tuple-element.127) | copy-start | bytes 3145732 | tf_op jit(solution)/shard_map/while/body/eval_jaxpr/cond
  209.8 1.0 copy-start.4
  218.1 8.7 %copy-start.2 = (bf16[128,4,4,128]{3,0,2,1:T(8,128)(2,1)S(1)}, bf16[128,4,4,128]{3,0,2,1:T(8,128)(2,1)}, u32[]{:S(2)}) copy-start(bf16[128,4,4,128]{3,0,2,1:T(8,128)(2,1)} %get-tuple-element.466) | copy-start | bytes 1572868 | tf_op jit(solution)/shard_map/while
  218.4 4.5 %copy-start.5 = (f32[4,4,128,128]{3,2,1,0:T(8,128)S(1)}, f32[4,4,128,128]{3,2,1,0:T(8,128)}, u32[]{:S(2)}) copy-start(f32[4,4,128,128]{3,2,1,0:T(8,128)} %get-tuple-element.119) | copy-start | bytes 3145732 | tf_op jit(solution)/shard_map/while/body/eval_jaxpr/cond
  225.8 1.0 copy-start.6
  227.0 3.4 %copy-start.3 = (f32[4,4,128,128]{3,2,1,0:T(8,128)S(1)}, f32[4,4,128,128]{3,2,1,0:T(8,128)}, u32[]{:S(2)}) copy-start(f32[4,4,128,128]{3,2,1,0:T(8,128)} %get-tuple-element.127) | copy-start | bytes 3145732 | tf_op jit(solution)/shard_map/while/body/eval_jaxpr/cond
  233.3 1.0 copy-start.4
  241.7 8.7 %copy-start.2 = (bf16[128,4,4,128]{3,0,2,1:T(8,128)(2,1)S(1)}, bf16[128,4,4,128]{3,0,2,1:T(8,128)(2,1)}, u32[]{:S(2)}) copy-start(bf16[128,4,4,128]{3,0,2,1:T(8,128)(2,1)} %get-tuple-element.466) | copy-start | bytes 1572868 | tf_op jit(solution)/shard_map/while
  241.9 4.5 %copy-start.5 = (f32[4,4,128,128]{3,2,1,0:T(8,128)S(1)}, f32[4,4,128,128]{3,2,1,0:T(8,128)}, u32[]{:S(2)}) copy-start(f32[4,4,128,128]{3,2,1,0:T(8,128)} %get-tuple-element.119) | copy-start | bytes 3145732 | tf_op jit(solution)/shard_map/while/body/eval_jaxpr/cond
  249.4 1.0 copy-start.6
  250.5 3.4 %copy-start.3 = (f32[4,4,128,128]{3,2,1,0:T(8,128)S(1)}, f32[4,4,128,128]{3,2,1,0:T(8,128)}, u32[]{:S(2)}) copy-start(f32[4,4,128,128]{3,2,1,0:T(8,128)} %get-tuple-element.127) | copy-start | bytes 3145732 | tf_op jit(solution)/shard_map/while/body/eval_jaxpr/cond
  256.9 1.0 copy-start.4
  265.2 8.7 %copy-start.2 = (bf16[128,4,4,128]{3,0,2,1:T(8,128)(2,1)S(1)}, bf16[128,4,4,128]{3,0,2,1:T(8,128)(2,1)}, u32[]{:S(2)}) copy-start(bf16[128,4,4,128]{3,0,2,1:T(8,128)(2,1)} %get-tuple-element.466) | copy-start | bytes 1572868 | tf_op jit(solution)/shard_map/while
  265.4 4.5 %copy-start.5 = (f32[4,4,128,128]{3,2,1,0:T(8,128)S(1)}, f32[4,4,128,128]{3,2,1,0:T(8,128)}, u32[]{:S(2)}) copy-start(f32[4,4,128,128]{3,2,1,0:T(8,128)} %get-tuple-element.119) | copy-start | bytes 3145732 | tf_op jit(solution)/shard_map/while/body/eval_jaxpr/cond
  272.9 1.0 copy-start.6
  274.1 3.4 %copy-start.3 = (f32[4,4,128,128]{3,2,1,0:T(8,128)S(1)}, f32[4,4,128,128]{3,2,1,0:T(8,128)}, u32[]{:S(2)}) copy-start(f32[4,4,128,128]{3,2,1,0:T(8,128)} %get-tuple-element.127) | copy-start | bytes 3145732 | tf_op jit(solution)/shard_map/while/body/eval_jaxpr/cond
  280.4 1.0 copy-start.4
  281.4 4.6 %copy-start.1 = (bf16[256,4096]{1,0:T(8,128)(2,1)S(1)}, bf16[256,4096]{1,0:T(8,128)(2,1)}, u32[]{:S(2)}) copy-start(bf16[256,4096]{1,0:T(8,128)(2,1)} %param.11) | copy-start | bytes 6291460
Sparse Core Ops, SparseCore 0:
  49.8 135.2 all-gather.1
where the time goes:
time: 294 us; the launch traced here: 293 us
  waiting for transfers between devices  131 us (45%)
  local copies, waits for them, and re-layouts  55.9 us (19%)
  matrix products  46.7 us (16%)
  other arithmetic  23.3 us (8%)
  between operations  14.2 us (5%)
  loops' own time  12.5 us (4%)
  blocking collectives  9.51 us (3%)
    all_gather x1, waiting for transfers between devices, body(): piece = lax.all_gather(kv_local, 'ctx', axis=0, tiled=True)  131 us
    dot_general x8, matrix products, attend(): jnp.einsum('grtn,ngd->grtd', weight.astype(jnp.bfloat16), value_block, pr...  23.4 us
    reduce_sum x8, other arithmetic, attend(): sums = sums * factor + jnp.sum(weight, axis=-1)  16 us
    dot_general x8, matrix products, attend(): jnp.einsum('tgrd,ngd->grtn', span_grid, key_block, preferred_element_type...  15 us
    another operation x1, loops' own time, body(): carry, _ = lax.scan(visit, carry, jnp.arange(blocks, dtype=jnp.int32))  11.9 us
    reshape x1, local copies, waits for them, and re-layouts, body(): key_matrix.reshape(key_matrix.shape[0], KEY_VALUE_HEADS, HEAD_SIZE)  11.7 us
    reshape x1, local copies, waits for them, and re-layouts, body(): value_matrix.reshape(value_matrix.shape[0], KEY_VALUE_HEADS, HEAD_SIZE)  11.3 us
    unnamed x1, blocking collectives  9.51 us
  transfers between devices with their start and end apart: 1, of which 1 were waited for; matrix products, arithmetic and copies ran while one was open for 2% of the time, Pallas kernels for 0%

commit v1 on v0

--- a/solution.py
+++ b/solution.py
@@ -51,7 +51,12 @@
         )
 
     carry = (fresh(), fresh())
-    piece = lax.all_gather(kv_local, "ctx", axis=0, tiled=True)
+    ring = [kv_local]
+    for hop in range(15):
+        ring.append(lax.ppermute(ring[-1], "ctx", [(dev, (dev + 1) % 16) for dev in range(16)]))
+    piece = jnp.roll(
+        jnp.concatenate(ring[::-1], axis=0), (lax.axis_index("ctx") + 1) * ring[0].shape[0], axis=0
+    )
     rows = piece.shape[0]
     width = math.gcd(rows, 1024)
     blocks = rows // width

time: 294 us -> 430 us (1.46)
  the two profiles are of different devices: /device:TPU:5 before, /device:TPU:30 now
where the time goes in v1:
time: 430 us; the launch traced here: 428 us
  waiting for transfers between devices  131 us (30%)
  local copies, waits for them, and re-layouts  116 us (27%)
  starting transfers between devices  83 us (19%)
  matrix products  50.2 us (12%)
  other arithmetic  23.8 us (6%)
  loops' own time  13.6 us (3%)
  blocking collectives  8.98 us (2%)
    ppermute x15, waiting for transfers between devices, body(): lax.ppermute(ring[-1], 'ctx', [(dev, (dev + 1) % 16) for dev in range(16)])  131 us
    ppermute x15, starting transfers between devices, body(): lax.ppermute(ring[-1], 'ctx', [(dev, (dev + 1) % 16) for dev in range(16)])  83 us
    unnamed x70, local copies, waits for them, and re-layouts  50.6 us
    dot_general x8, matrix products, attend(): jnp.einsum('grtn,ngd->grtd', weight.astype(jnp.bfloat16), value_block, pr...  23.4 us
    reduce_sum x8, other arithmetic, attend(): sums = sums * factor + jnp.sum(weight, axis=-1)  16 us
    dot_general x8, matrix products, attend(): jnp.einsum('tgrd,ngd->grtn', span_grid, key_block, preferred_element_type...  15.3 us
    another operation x1, loops' own time, body(): carry, _ = lax.scan(visit, carry, jnp.arange(blocks, dtype=jnp.int32))  12.9 us
    reshape x1, local copies, waits for them, and re-layouts, body(): key_matrix.reshape(key_matrix.shape[0], KEY_VALUE_HEADS, HEAD_SIZE)  11.5 us
  transfers between devices with their start and end apart: 15, of which 15 were waited for; matrix products, arithmetic and copies ran while one was open for 3% of the time, Pallas kernels for 0%

profile of v1, /device:TPU:30, one launch (start us, length us, event | category | flops | bytes accessed | tf_op | source)
XLA Modules:
  0.0 427.8 jit_solution(15971153695580275489)
XLA Ops:
  0.0 11.5 %copy.48 = bf16[4096,1024]{0,1:T(8,128)(2,1)} copy(bf16[4096,1024]{1,0:T(8,128)(2,1)} %param.13) | data formatting | bytes 16777216 | tf_op jit(solution)/shard_map/reshape | solution.py:19
  11.5 11.2 %copy.49 = bf16[4096,1024]{0,1:T(8,128)(2,1)} copy(bf16[4096,1024]{1,0:T(8,128)(2,1)} %param.14) | data formatting | bytes 16777216 | tf_op jit(solution)/shard_map/reshape | solution.py:20
  22.7 5.8 %fusion.34 = f32[8,1,256,128]{2,3,0,1:T(8,128)S(1)} fusion(bf16[4096,8,128]{0,2,1:T(8,128)(2,1)} %bitcast.118, bf16[256,4096]{1,0:T(8,128)(2,1)S(1)} %copy-done), kind=kOutput, calls=%fused_computation.41 | convolution fusion | flops 2147483648 | bytes 11534336 | tf_op jit(solution)/shard_map/tc,chd->htd/dot_general | solution.py:22
  28.5 5.8 %fusion.37 = f32[8,1,256,128]{2,3,0,1:T(8,128)S(1)} fusion(bf16[4096,8,128]{0,2,1:T(8,128)(2,1)} %bitcast.117, bf16[256,4096]{1,0:T(8,128)(2,1)S(1)} %copy-done), kind=kOutput, calls=%fused_computation.42 | convolution fusion | flops 2147483648 | bytes 11534336 | tf_op jit(solution)/shard_map/tc,chd->htd/dot_general | solution.py:25
  34.5 9.0 %all-reduce.2 = bf16[8,2,256,128]{2,3,0,1:T(8,128)(2,1)S(1)} all-reduce(f32[8,2,256,128]{2,3,0,1:T(8,128)S(1)} %pad_maximum_fusion), channel_id=2, replica_groups=mesh['ctx'=16,'tp'=2] {'tp'}, use_global_device_ids=true, to_apply=%region_0.0.clone | all-reduce | flops 524288 | bytes 3145728
  44.8 14.2 %collective-permute-done = bf16[256,4,2,128]{0,3,1,2:T(8,128)(2,1)S(1)} collective-permute-done((bf16[256,4,2,128]{0,3,1,2:T(8,128)(2,1)S(1)}, bf16[256,4,2,128]{0,3,1,2:T(8,128)(2,1)S(1)}, u32[]{:S(2)}, u32[]{:S(2)}) %collective-permute-start) | collective-permute-done | bytes 524320 | tf_op jit(solution)/shard_map/ppermute | solution.py:56
  59.0 3.9 collective-permute-start.1
  62.9 11.1 %collective-permute-done.1 = bf16[256,4,2,128]{0,3,1,2:T(8,128)(2,1)S(1)} collective-permute-done((bf16[256,4,2,128]{0,3,1,2:T(8,128)(2,1)S(1)}, bf16[256,4,2,128]{0,3,1,2:T(8,128)(2,1)S(1)}, u32[]{:S(2)}, u32[]{:S(2)}) %collective-permute-start.1) | collective-permute-done | bytes 524320 | tf_op jit(solution)/shard_map/ppermute | solution.py:56
  74.0 6.1 %collective-permute-start.2 = (bf16[256,4,2,128]{0,3,1,2:T(8,128)(2,1)S(1)}, bf16[256,4,2,128]{0,3,1,2:T(8,128)(2,1)S(1)}, u32[]{:S(2)}, u32[]{:S(2)}) collective-permute-start(bf16[256,4,2,128]{0,3,1,2:T(8,128)(2,1)S(1)} %collective-permute-done.1), channel_id=1, source_target_pairs={{0,2},{2,4},{4,6},{6,8},{8,10},{10,12},{12,14},{14,16},{16,18},{18... | collective-permute-start | bytes 1572872 | tf_op jit(solution)/shard_map/ppermute | solution.py:56
  80.1 10.3 %collective-permute-done.2 = bf16[256,4,2,128]{0,3,1,2:T(8,128)(2,1)S(1)} collective-permute-done((bf16[256,4,2,128]{0,3,1,2:T(8,128)(2,1)S(1)}, bf16[256,4,2,128]{0,3,1,2:T(8,128)(2,1)S(1)}, u32[]{:S(2)}, u32[]{:S(2)}) %collective-permute-start.2) | collective-permute-done | bytes 524320 | tf_op jit(solution)/shard_map/ppermute | solution.py:56
  90.4 6.1 %collective-permute-start.3 = (bf16[256,4,2,128]{0,3,1,2:T(8,128)(2,1)S(1)}, bf16[256,4,2,128]{0,3,1,2:T(8,128)(2,1)S(1)}, u32[]{:S(2)}, u32[]{:S(2)}) collective-permute-start(bf16[256,4,2,128]{0,3,1,2:T(8,128)(2,1)S(1)} %collective-permute-done.2), channel_id=1, source_target_pairs={{0,2},{2,4},{4,6},{6,8},{8,10},{10,12},{12,14},{14,16},{16,18},{18... | collective-permute-start | bytes 1572872 | tf_op jit(solution)/shard_map/ppermute | solution.py:56
  96.5 9.4 %collective-permute-done.3 = bf16[256,4,2,128]{0,3,1,2:T(8,128)(2,1)S(1)} collective-permute-done((bf16[256,4,2,128]{0,3,1,2:T(8,128)(2,1)S(1)}, bf16[256,4,2,128]{0,3,1,2:T(8,128)(2,1)S(1)}, u32[]{:S(2)}, u32[]{:S(2)}) %collective-permute-start.3) | collective-permute-done | bytes 524320 | tf_op jit(solution)/shard_map/ppermute | solution.py:56
  105.9 6.1 %collective-permute-start.4 = (bf16[256,4,2,128]{0,3,1,2:T(8,128)(2,1)S(1)}, bf16[256,4,2,128]{0,3,1,2:T(8,128)(2,1)S(1)}, u32[]{:S(2)}, u32[]{:S(2)}) collective-permute-start(bf16[256,4,2,128]{0,3,1,2:T(8,128)(2,1)S(1)} %collective-permute-done.3), channel_id=1, source_target_pairs={{0,2},{2,4},{4,6},{6,8},{8,10},{10,12},{12,14},{14,16},{16,18},{18... | collective-permute-start | bytes 1572872 | tf_op jit(solution)/shard_map/ppermute | solution.py:56
  112.0 8.6 %collective-permute-done.4 = bf16[256,4,2,128]{0,3,1,2:T(8,128)(2,1)S(1)} collective-permute-done((bf16[256,4,2,128]{0,3,1,2:T(8,128)(2,1)S(1)}, bf16[256,4,2,128]{0,3,1,2:T(8,128)(2,1)S(1)}, u32[]{:S(2)}, u32[]{:S(2)}) %collective-permute-start.4) | collective-permute-done | bytes 524320 | tf_op jit(solution)/shard_map/ppermute | solution.py:56
  121.3 6.1 %collective-permute-start.5 = (bf16[256,4,2,128]{0,3,1,2:T(8,128)(2,1)S(1)}, bf16[256,4,2,128]{0,3,1,2:T(8,128)(2,1)S(1)}, u32[]{:S(2)}, u32[]{:S(2)}) collective-permute-start(bf16[256,4,2,128]{0,3,1,2:T(8,128)(2,1)S(1)} %collective-permute-done.4), channel_id=1, source_target_pairs={{0,2},{2,4},{4,6},{6,8},{8,10},{10,12},{12,14},{14,16},{16,18},{18... | collective-permute-start | bytes 1572872 | tf_op jit(solution)/shard_map/ppermute | solution.py:56
  127.4 7.7 %collective-permute-done.5 = bf16[256,4,2,128]{0,3,1,2:T(8,128)(2,1)S(1)} collective-permute-done((bf16[256,4,2,128]{0,3,1,2:T(8,128)(2,1)S(1)}, bf16[256,4,2,128]{0,3,1,2:T(8,128)(2,1)S(1)}, u32[]{:S(2)}, u32[]{:S(2)}) %collective-permute-start.5) | collective-permute-done | bytes 524320 | tf_op jit(solution)/shard_map/ppermute | solution.py:56
  135.9 6.1 %collective-permute-start.6 = (bf16[256,4,2,128]{0,3,1,2:T(8,128)(2,1)S(1)}, bf16[256,4,2,128]{0,3,1,2:T(8,128)(2,1)S(1)}, u32[]{:S(2)}, u32[]{:S(2)}) collective-permute-start(bf16[256,4,2,128]{0,3,1,2:T(8,128)(2,1)S(1)} %collective-permute-done.5), channel_id=1, source_target_pairs={{0,2},{2,4},{4,6},{6,8},{8,10},{10,12},{12,14},{14,16},{16,18},{18... | collective-permute-start | bytes 1572872 | tf_op jit(solution)/shard_map/ppermute | solution.py:56
  142.0 6.9 %collective-permute-done.6 = bf16[256,4,2,128]{0,3,1,2:T(8,128)(2,1)S(1)} collective-permute-done((bf16[256,4,2,128]{0,3,1,2:T(8,128)(2,1)S(1)}, bf16[256,4,2,128]{0,3,1,2:T(8,128)(2,1)S(1)}, u32[]{:S(2)}, u32[]{:S(2)}) %collective-permute-start.6) | collective-permute-done | bytes 524320 | tf_op jit(solution)/shard_map/ppermute | solution.py:56
  149.7 6.1 %collective-permute-start.7 = (bf16[256,4,2,128]{0,3,1,2:T(8,128)(2,1)S(1)}, bf16[256,4,2,128]{0,3,1,2:T(8,128)(2,1)S(1)}, u32[]{:S(2)}, u32[]{:S(2)}) collective-permute-start(bf16[256,4,2,128]{0,3,1,2:T(8,128)(2,1)S(1)} %collective-permute-done.6), channel_id=1, source_target_pairs={{0,2},{2,4},{4,6},{6,8},{8,10},{10,12},{12,14},{14,16},{16,18},{18... | collective-permute-start | bytes 1572872 | tf_op jit(solution)/shard_map/ppermute | solution.py:56
  155.8 6.7 %collective-permute-done.7 = bf16[256,4,2,128]{0,3,1,2:T(8,128)(2,1)S(1)} collective-permute-done((bf16[256,4,2,128]{0,3,1,2:T(8,128)(2,1)S(1)}, bf16[256,4,2,128]{0,3,1,2:T(8,128)(2,1)S(1)}, u32[]{:S(2)}, u32[]{:S(2)}) %collective-permute-start.7) | collective-permute-done | bytes 524320 | tf_op jit(solution)/shard_map/ppermute | solution.py:56
  163.3 6.1 %collective-permute-start.8 = (bf16[256,4,2,128]{0,3,1,2:T(8,128)(2,1)S(1)}, bf16[256,4,2,128]{0,3,1,2:T(8,128)(2,1)S(1)}, u32[]{:S(2)}, u32[]{:S(2)}) collective-permute-start(bf16[256,4,2,128]{0,3,1,2:T(8,128)(2,1)S(1)} %collective-permute-done.7), channel_id=1, source_target_pairs={{0,2},{2,4},{4,6},{6,8},{8,10},{10,12},{12,14},{14,16},{16,18},{18... | collective-permute-start | bytes 1572872 | tf_op jit(solution)/shard_map/ppermute | solution.py:56
  169.3 7.3 %collective-permute-done.8 = bf16[256,4,2,128]{0,3,1,2:T(8,128)(2,1)S(1)} collective-permute-done((bf16[256,4,2,128]{0,3,1,2:T(8,128)(2,1)S(1)}, bf16[256,4,2,128]{0,3,1,2:T(8,128)(2,1)S(1)}, u32[]{:S(2)}, u32[]{:S(2)}) %collective-permute-start.8) | collective-permute-done | bytes 524320 | tf_op jit(solution)/shard_map/ppermute | solution.py:56
  177.5 6.1 %collective-permute-start.9 = (bf16[256,4,2,128]{0,3,1,2:T(8,128)(2,1)S(1)}, bf16[256,4,2,128]{0,3,1,2:T(8,128)(2,1)S(1)}, u32[]{:S(2)}, u32[]{:S(2)}) collective-permute-start(bf16[256,4,2,128]{0,3,1,2:T(8,128)(2,1)S(1)} %collective-permute-done.8), channel_id=1, source_target_pairs={{0,2},{2,4},{4,6},{6,8},{8,10},{10,12},{12,14},{14,16},{16,18},{18... | collective-permute-start | bytes 1572872 | tf_op jit(solution)/shard_map/ppermute | solution.py:56
  183.6 8.5 %collective-permute-done.9 = bf16[256,4,2,128]{0,3,1,2:T(8,128)(2,1)S(1)} collective-permute-done((bf16[256,4,2,128]{0,3,1,2:T(8,128)(2,1)S(1)}, bf16[256,4,2,128]{0,3,1,2:T(8,128)(2,1)S(1)}, u32[]{:S(2)}, u32[]{:S(2)}) %collective-permute-start.9) | collective-permute-done | bytes 524320 | tf_op jit(solution)/shard_map/ppermute | solution.py:56
  192.9 6.1 %collective-permute-start.10 = (bf16[256,4,2,128]{0,3,1,2:T(8,128)(2,1)S(1)}, bf16[256,4,2,128]{0,3,1,2:T(8,128)(2,1)S(1)}, u32[]{:S(2)}, u32[]{:S(2)}) collective-permute-start(bf16[256,4,2,128]{0,3,1,2:T(8,128)(2,1)S(1)} %collective-permute-done.9), channel_id=1, source_target_pairs={{0,2},{2,4},{4,6},{6,8},{8,10},{10,12},{12,14},{14,16},{16,18},{18... | collective-permute-start | bytes 1572872 | tf_op jit(solution)/shard_map/ppermute | solution.py:56
  198.9 9.7 %collective-permute-done.10 = bf16[256,4,2,128]{0,3,1,2:T(8,128)(2,1)S(1)} collective-permute-done((bf16[256,4,2,128]{0,3,1,2:T(8,128)(2,1)S(1)}, bf16[256,4,2,128]{0,3,1,2:T(8,128)(2,1)S(1)}, u32[]{:S(2)}, u32[]{:S(2)}) %collective-permute-start.10) | collective-permute-done | bytes 524320 | tf_op jit(solution)/shard_map/ppermute | solution.py:56
  209.4 6.1 %collective-permute-start.11 = (bf16[256,4,2,128]{0,3,1,2:T(8,128)(2,1)S(1)}, bf16[256,4,2,128]{0,3,1,2:T(8,128)(2,1)}, u32[]{:S(2)}, u32[]{:S(2)}) collective-permute-start(bf16[256,4,2,128]{0,3,1,2:T(8,128)(2,1)S(1)} %collective-permute-done.10), channel_id=1, source_target_pairs={{0,2},{2,4},{4,6},{6,8},{8,10},{10,12},{12,14},{14,16},{16,18},{18... | collective-permute-start | bytes 1572872 | tf_op jit(solution)/shard_map/ppermute | solution.py:56
  215.5 11.3 %collective-permute-done.11 = bf16[256,4,2,128]{0,3,1,2:T(8,128)(2,1)} collective-permute-done((bf16[256,4,2,128]{0,3,1,2:T(8,128)(2,1)S(1)}, bf16[256,4,2,128]{0,3,1,2:T(8,128)(2,1)}, u32[]{:S(2)}, u32[]{:S(2)}) %collective-permute-start.11) | collective-permute-done | bytes 524320 | tf_op jit(solution)/shard_map/ppermute | solution.py:56
  226.7 6.2 %collective-permute-start.12 = (bf16[256,4,2,128]{0,3,1,2:T(8,128)(2,1)}, bf16[256,4,2,128]{0,3,1,2:T(8,128)(2,1)}, u32[]{:S(2)}, u32[]{:S(2)}) collective-permute-start(bf16[256,4,2,128]{0,3,1,2:T(8,128)(2,1)} %collective-permute-done.11), channel_id=1, source_target_pairs={{0,2},{2,4},{4,6},{6,8},{8,10},{10,12},{12,14},{14,16},{16,18},{18... | collective-permute-start | bytes 1572872 | tf_op jit(solution)/shard_map/ppermute | solution.py:56
  232.9 12.5 %collective-permute-done.12 = bf16[256,4,2,128]{0,3,1,2:T(8,128)(2,1)} collective-permute-done((bf16[256,4,2,128]{0,3,1,2:T(8,128)(2,1)}, bf16[256,4,2,128]{0,3,1,2:T(8,128)(2,1)}, u32[]{:S(2)}, u32[]{:S(2)}) %collective-permute-start.12) | collective-permute-done | bytes 524320 | tf_op jit(solution)/shard_map/ppermute | solution.py:56
  245.4 6.1 %collective-permute-start.13 = (bf16[256,4,2,128]{0,3,1,2:T(8,128)(2,1)}, bf16[256,4,2,128]{0,3,1,2:T(8,128)(2,1)}, u32[]{:S(2)}, u32[]{:S(2)}) collective-permute-start(bf16[256,4,2,128]{0,3,1,2:T(8,128)(2,1)} %collective-permute-done.12), channel_id=1, source_target_pairs={{0,2},{2,4},{4,6},{6,8},{8,10},{10,12},{12,14},{14,16},{16,18},{18... | collective-permute-start | bytes 1572872 | tf_op jit(solution)/shard_map/ppermute | solution.py:56
  263.2 6.1 %collective-permute-start.14 = (bf16[256,4,2,128]{0,3,1,2:T(8,128)(2,1)}, bf16[256,4,2,128]{0,3,1,2:T(8,128)(2,1)S(1)}, u32[]{:S(2)}, u32[]{:S(2)}) collective-permute-start(bf16[256,4,2,128]{0,3,1,2:T(8,128)(2,1)} %collective-permute-done.13), channel_id=1, source_target_pairs={{0,2},{2,4},{4,6},{6,8},{8,10},{10,12},{12,14},{14,16},{16,18},{18... | collective-permute-start | bytes 1572872 | tf_op jit(solution)/shard_map/ppermute | solution.py:56
  270.2 6.0 %collective-permute-done.14 = bf16[256,4,2,128]{0,3,1,2:T(8,128)(2,1)S(1)} collective-permute-done((bf16[256,4,2,128]{0,3,1,2:T(8,128)(2,1)}, bf16[256,4,2,128]{0,3,1,2:T(8,128)(2,1)S(1)}, u32[]{:S(2)}, u32[]{:S(2)}) %collective-permute-start.14) | collective-permute-done | bytes 524320 | tf_op jit(solution)/shard_map/ppermute | solution.py:56
  317.4 7.8 %constant_dynamic-slice_fusion.2 = bf16[4096,4,2,128]{0,3,1,2:T(8,128)(2,1)} fusion(bf16[8192,4,2,128]{0,3,1,2:T(8,128)(2,1)} %constant_dynamic-update-slice_fusion, s32[]{:T(128)S(6)} %select_n.57), kind=kLoop, calls=%fused_computation.94 | loop fusion | bytes 16777220 | tf_op jit(solution)/shard_map/jit(_roll_dynamic)/dynamic_slice | solution.py:57
  327.4 95.8 %while.20 = (s32[]{:T(128)}, f32[4,4,128]{2,1,0:T(4,128)S(1)}, f32[4,4,128]{2,1,0:T(4,128)S(1)}, f32[4,4,128,128]{3,2,1,0:T(8,128)}, f32[4,4,128]{2,1,0:T(4,128)...) while((s32[]{:T(128)}, f32[4,4,128]{2,1,0:T(4,128)S(1)}, ...), condition=%wide.region_14.15_spmd, body=%wide.region_4.14_spmd.sunk | while | flops 2203329536 | bytes 88360616 | solution.py:105
  334.1 8.8 %conditional.5 = ((f32[4,4,128]{2,1,0:T(4,128)S(1)}, f32[4,4,128]{2,1,0:T(4,128)S(1)}, f32[4,4,128,128]{3,2,1,0:T(8,128)})) conditional(s32[]{:T(128)} %convert_element_type.39, (f32[4,4,128]{2,1,0:T(4,128)S(1)}, f32[4,4,128]{2,1,0:T(4,128)S(1)}, f32[4,4,128,128]{3,2,1,0:T(8,128)}) %tuple.59, (s32[1024]{0:T(1024)S(1)}, s32[128]{0:T(128)S(1)}, ...), branch_computations={%region_10.10_spmd, %region_11.13_spmd} | conditional | flops 1101664256 | bytes 38933080 | solution.py:102
  338.9 2.9 fusion.21
  344.0 7.5 %conditional.4 = ((f32[4,4,128]{2,1,0:T(4,128)S(1)}, f32[4,4,128]{2,1,0:T(4,128)S(1)}, f32[4,4,128,128]{3,2,1,0:T(8,128)})) conditional(s32[]{:T(128)} %convert_element_type.38, (f32[4,4,128]{2,1,0:T(4,128)S(1)}, f32[4,4,128]{2,1,0:T(4,128)S(1)}, f32[4,4,128,128]{3,2,1,0:T(8,128)}) %tuple.57, (s32[1024]{0:T(1024)S(1)}, s32[128]{0:T(128)S(1)}, ...), branch_computations={%region_6.6_spmd, %region_7.9_spmd} | conditional | flops 1101664256 | bytes 38933080 | solution.py:102
  347.6 2.9 fusion.6
  358.0 8.8 %conditional.5 = ((f32[4,4,128]{2,1,0:T(4,128)S(1)}, f32[4,4,128]{2,1,0:T(4,128)S(1)}, f32[4,4,128,128]{3,2,1,0:T(8,128)})) conditional(s32[]{:T(128)} %convert_element_type.39, (f32[4,4,128]{2,1,0:T(4,128)S(1)}, f32[4,4,128]{2,1,0:T(4,128)S(1)}, f32[4,4,128,128]{3,2,1,0:T(8,128)}) %tuple.59, (s32[1024]{0:T(1024)S(1)}, s32[128]{0:T(128)S(1)}, ...), branch_computations={%region_10.10_spmd, %region_11.13_spmd} | conditional | flops 1101664256 | bytes 38933080 | solution.py:102
  362.8 2.9 fusion.21
  367.9 7.5 %conditional.4 = ((f32[4,4,128]{2,1,0:T(4,128)S(1)}, f32[4,4,128]{2,1,0:T(4,128)S(1)}, f32[4,4,128,128]{3,2,1,0:T(8,128)})) conditional(s32[]{:T(128)} %convert_element_type.38, (f32[4,4,128]{2,1,0:T(4,128)S(1)}, f32[4,4,128]{2,1,0:T(4,128)S(1)}, f32[4,4,128,128]{3,2,1,0:T(8,128)}) %tuple.57, (s32[1024]{0:T(1024)S(1)}, s32[128]{0:T(128)S(1)}, ...), branch_computations={%region_6.6_spmd, %region_7.9_spmd} | conditional | flops 1101664256 | bytes 38933080 | solution.py:102
  381.9 8.8 %conditional.5 = ((f32[4,4,128]{2,1,0:T(4,128)S(1)}, f32[4,4,128]{2,1,0:T(4,128)S(1)}, f32[4,4,128,128]{3,2,1,0:T(8,128)})) conditional(s32[]{:T(128)} %convert_element_type.39, (f32[4,4,128]{2,1,0:T(4,128)S(1)}, f32[4,4,128]{2,1,0:T(4,128)S(1)}, f32[4,4,128,128]{3,2,1,0:T(8,128)}) %tuple.59, (s32[1024]{0:T(1024)S(1)}, s32[128]{0:T(128)S(1)}, ...), branch_computations={%region_10.10_spmd, %region_11.13_spmd} | conditional | flops 1101664256 | bytes 38933080 | solution.py:102
  386.7 2.9 fusion.21
  391.8 7.5 %conditional.4 = ((f32[4,4,128]{2,1,0:T(4,128)S(1)}, f32[4,4,128]{2,1,0:T(4,128)S(1)}, f32[4,4,128,128]{3,2,1,0:T(8,128)})) conditional(s32[]{:T(128)} %convert_element_type.38, (f32[4,4,128]{2,1,0:T(4,128)S(1)}, f32[4,4,128]{2,1,0:T(4,128)S(1)}, f32[4,4,128,128]{3,2,1,0:T(8,128)}) %tuple.57, (s32[1024]{0:T(1024)S(1)}, s32[128]{0:T(128)S(1)}, ...), branch_computations={%region_6.6_spmd, %region_7.9_spmd} | conditional | flops 1101664256 | bytes 38933080 | solution.py:102
  405.8 8.8 %conditional.5 = ((f32[4,4,128]{2,1,0:T(4,128)S(1)}, f32[4,4,128]{2,1,0:T(4,128)S(1)}, f32[4,4,128,128]{3,2,1,0:T(8,128)})) conditional(s32[]{:T(128)} %convert_element_type.39, (f32[4,4,128]{2,1,0:T(4,128)S(1)}, f32[4,4,128]{2,1,0:T(4,128)S(1)}, f32[4,4,128,128]{3,2,1,0:T(8,128)}) %tuple.59, (s32[1024]{0:T(1024)S(1)}, s32[128]{0:T(128)S(1)}, ...), branch_computations={%region_10.10_spmd, %region_11.13_spmd} | conditional | flops 1101664256 | bytes 38933080 | solution.py:102
  410.6 2.9 fusion.21
  415.7 7.5 %conditional.4 = ((f32[4,4,128]{2,1,0:T(4,128)S(1)}, f32[4,4,128]{2,1,0:T(4,128)S(1)}, f32[4,4,128,128]{3,2,1,0:T(8,128)})) conditional(s32[]{:T(128)} %convert_element_type.38, (f32[4,4,128]{2,1,0:T(4,128)S(1)}, f32[4,4,128]{2,1,0:T(4,128)S(1)}, f32[4,4,128,128]{3,2,1,0:T(8,128)}) %tuple.57, (s32[1024]{0:T(1024)S(1)}, s32[128]{0:T(128)S(1)}, ...), branch_computations={%region_6.6_spmd, %region_7.9_spmd} | conditional | flops 1101664256 | bytes 38933080 | solution.py:102
  (205 shorter events, 134.6 us)
Async XLA Ops:
  0.0 22.7 %copy-start = (bf16[256,4096]{1,0:T(8,128)(2,1)S(1)}, bf16[256,4096]{1,0:T(8,128)(2,1)}, u32[]{:S(2)}) copy-start(bf16[256,4096]{1,0:T(8,128)(2,1)} %param.11) | copy-start | bytes 6291460
  22.7 20.7 %copy-start.22 = (u32[32]{0:T(128)S(1)}, u32[32]{0:T(128)}, u32[]{:S(2)}) copy-start(u32[32]{0:T(128)} %constant.102) | copy-start | bytes 388
  28.5 240.8 %copy-start.21 = (s32[32]{0:T(128)S(1)}, s32[32]{0:T(128)}, u32[]{:S(2)}) copy-start(s32[32]{0:T(128)} %param.15) | copy-start | bytes 388
  44.7 14.3 %collective-permute-start = (bf16[256,4,2,128]{0,3,1,2:T(8,128)(2,1)S(1)}, bf16[256,4,2,128]{0,3,1,2:T(8,128)(2,1)S(1)}, u32[]{:S(2)}, u32[]{:S(2)}) collective-permute-start(bf16[256,4,2,128]{0,3,1,2:T(8,128)(2,1)S(1)} %fusion.40), channel_id=1, source_target_pairs={{0,2},{2,4},{4,6},{6,8},{8,10},{10,12},{12,14},{14,16},{16,18},{18... | collective-permute-start | bytes 1572872 | tf_op jit(solution)/shard_map/ppermute | solution.py:56
  59.0 15.0 %collective-permute-start.1 = (bf16[256,4,2,128]{0,3,1,2:T(8,128)(2,1)S(1)}, bf16[256,4,2,128]{0,3,1,2:T(8,128)(2,1)S(1)}, u32[]{:S(2)}, u32[]{:S(2)}) collective-permute-start(bf16[256,4,2,128]{0,3,1,2:T(8,128)(2,1)S(1)} %collective-permute-done), channel_id=1, source_target_pairs={{0,2},{2,4},{4,6},{6,8},{8,10},{10,12},{12,14},{14,16},{16,18},{18... | collective-permute-start | bytes 1572872 | tf_op jit(solution)/shard_map/ppermute | solution.py:56
  74.0 16.4 %collective-permute-start.2 = (bf16[256,4,2,128]{0,3,1,2:T(8,128)(2,1)S(1)}, bf16[256,4,2,128]{0,3,1,2:T(8,128)(2,1)S(1)}, u32[]{:S(2)}, u32[]{:S(2)}) collective-permute-start(bf16[256,4,2,128]{0,3,1,2:T(8,128)(2,1)S(1)} %collective-permute-done.1), channel_id=1, source_target_pairs={{0,2},{2,4},{4,6},{6,8},{8,10},{10,12},{12,14},{14,16},{16,18},{18... | collective-permute-start | bytes 1572872 | tf_op jit(solution)/shard_map/ppermute | solution.py:56
  90.4 15.5 %collective-permute-start.3 = (bf16[256,4,2,128]{0,3,1,2:T(8,128)(2,1)S(1)}, bf16[256,4,2,128]{0,3,1,2:T(8,128)(2,1)S(1)}, u32[]{:S(2)}, u32[]{:S(2)}) collective-permute-start(bf16[256,4,2,128]{0,3,1,2:T(8,128)(2,1)S(1)} %collective-permute-done.2), channel_id=1, source_target_pairs={{0,2},{2,4},{4,6},{6,8},{8,10},{10,12},{12,14},{14,16},{16,18},{18... | collective-permute-start | bytes 1572872 | tf_op jit(solution)/shard_map/ppermute | solution.py:56
  105.9 14.6 %collective-permute-start.4 = (bf16[256,4,2,128]{0,3,1,2:T(8,128)(2,1)S(1)}, bf16[256,4,2,128]{0,3,1,2:T(8,128)(2,1)S(1)}, u32[]{:S(2)}, u32[]{:S(2)}) collective-permute-start(bf16[256,4,2,128]{0,3,1,2:T(8,128)(2,1)S(1)} %collective-permute-done.3), channel_id=1, source_target_pairs={{0,2},{2,4},{4,6},{6,8},{8,10},{10,12},{12,14},{14,16},{16,18},{18... | collective-permute-start | bytes 1572872 | tf_op jit(solution)/shard_map/ppermute | solution.py:56
  120.5 0.8 copy-start.7
  121.3 13.8 %collective-permute-start.5 = (bf16[256,4,2,128]{0,3,1,2:T(8,128)(2,1)S(1)}, bf16[256,4,2,128]{0,3,1,2:T(8,128)(2,1)S(1)}, u32[]{:S(2)}, u32[]{:S(2)}) collective-permute-start(bf16[256,4,2,128]{0,3,1,2:T(8,128)(2,1)S(1)} %collective-permute-done.4), channel_id=1, source_target_pairs={{0,2},{2,4},{4,6},{6,8},{8,10},{10,12},{12,14},{14,16},{16,18},{18... | collective-permute-start | bytes 1572872 | tf_op jit(solution)/shard_map/ppermute | solution.py:56
  135.1 0.8 copy-start.9
  135.9 12.9 %collective-permute-start.6 = (bf16[256,4,2,128]{0,3,1,2:T(8,128)(2,1)S(1)}, bf16[256,4,2,128]{0,3,1,2:T(8,128)(2,1)S(1)}, u32[]{:S(2)}, u32[]{:S(2)}) collective-permute-start(bf16[256,4,2,128]{0,3,1,2:T(8,128)(2,1)S(1)} %collective-permute-done.5), channel_id=1, source_target_pairs={{0,2},{2,4},{4,6},{6,8},{8,10},{10,12},{12,14},{14,16},{16,18},{18... | collective-permute-start | bytes 1572872 | tf_op jit(solution)/shard_map/ppermute | solution.py:56
  149.7 12.8 %collective-permute-start.7 = (bf16[256,4,2,128]{0,3,1,2:T(8,128)(2,1)S(1)}, bf16[256,4,2,128]{0,3,1,2:T(8,128)(2,1)S(1)}, u32[]{:S(2)}, u32[]{:S(2)}) collective-permute-start(bf16[256,4,2,128]{0,3,1,2:T(8,128)(2,1)S(1)} %collective-permute-done.6), channel_id=1, source_target_pairs={{0,2},{2,4},{4,6},{6,8},{8,10},{10,12},{12,14},{14,16},{16,18},{18... | collective-permute-start | bytes 1572872 | tf_op jit(solution)/shard_map/ppermute | solution.py:56
  163.3 13.4 %collective-permute-start.8 = (bf16[256,4,2,128]{0,3,1,2:T(8,128)(2,1)S(1)}, bf16[256,4,2,128]{0,3,1,2:T(8,128)(2,1)S(1)}, u32[]{:S(2)}, u32[]{:S(2)}) collective-permute-start(bf16[256,4,2,128]{0,3,1,2:T(8,128)(2,1)S(1)} %collective-permute-done.7), channel_id=1, source_target_pairs={{0,2},{2,4},{4,6},{6,8},{8,10},{10,12},{12,14},{14,16},{16,18},{18... | collective-permute-start | bytes 1572872 | tf_op jit(solution)/shard_map/ppermute | solution.py:56
  177.5 14.6 %collective-permute-start.9 = (bf16[256,4,2,128]{0,3,1,2:T(8,128)(2,1)S(1)}, bf16[256,4,2,128]{0,3,1,2:T(8,128)(2,1)S(1)}, u32[]{:S(2)}, u32[]{:S(2)}) collective-permute-start(bf16[256,4,2,128]{0,3,1,2:T(8,128)(2,1)S(1)} %collective-permute-done.8), channel_id=1, source_target_pairs={{0,2},{2,4},{4,6},{6,8},{8,10},{10,12},{12,14},{14,16},{16,18},{18... | collective-permute-start | bytes 1572872 | tf_op jit(solution)/shard_map/ppermute | solution.py:56
  192.9 15.7 %collective-permute-start.10 = (bf16[256,4,2,128]{0,3,1,2:T(8,128)(2,1)S(1)}, bf16[256,4,2,128]{0,3,1,2:T(8,128)(2,1)S(1)}, u32[]{:S(2)}, u32[]{:S(2)}) collective-permute-start(bf16[256,4,2,128]{0,3,1,2:T(8,128)(2,1)S(1)} %collective-permute-done.9), channel_id=1, source_target_pairs={{0,2},{2,4},{4,6},{6,8},{8,10},{10,12},{12,14},{14,16},{16,18},{18... | collective-permute-start | bytes 1572872 | tf_op jit(solution)/shard_map/ppermute | solution.py:56
  209.4 17.4 %collective-permute-start.11 = (bf16[256,4,2,128]{0,3,1,2:T(8,128)(2,1)S(1)}, bf16[256,4,2,128]{0,3,1,2:T(8,128)(2,1)}, u32[]{:S(2)}, u32[]{:S(2)}) collective-permute-start(bf16[256,4,2,128]{0,3,1,2:T(8,128)(2,1)S(1)} %collective-permute-done.10), channel_id=1, source_target_pairs={{0,2},{2,4},{4,6},{6,8},{8,10},{10,12},{12,14},{14,16},{16,18},{18... | collective-permute-start | bytes 1572872 | tf_op jit(solution)/shard_map/ppermute | solution.py:56
  226.7 18.7 %collective-permute-start.12 = (bf16[256,4,2,128]{0,3,1,2:T(8,128)(2,1)}, bf16[256,4,2,128]{0,3,1,2:T(8,128)(2,1)}, u32[]{:S(2)}, u32[]{:S(2)}) collective-permute-start(bf16[256,4,2,128]{0,3,1,2:T(8,128)(2,1)} %collective-permute-done.11), channel_id=1, source_target_pairs={{0,2},{2,4},{4,6},{6,8},{8,10},{10,12},{12,14},{14,16},{16,18},{18... | collective-permute-start | bytes 1572872 | tf_op jit(solution)/shard_map/ppermute | solution.py:56
  245.4 17.7 %collective-permute-start.13 = (bf16[256,4,2,128]{0,3,1,2:T(8,128)(2,1)}, bf16[256,4,2,128]{0,3,1,2:T(8,128)(2,1)}, u32[]{:S(2)}, u32[]{:S(2)}) collective-permute-start(bf16[256,4,2,128]{0,3,1,2:T(8,128)(2,1)} %collective-permute-done.12), channel_id=1, source_target_pairs={{0,2},{2,4},{4,6},{6,8},{8,10},{10,12},{12,14},{14,16},{16,18},{18... | collective-permute-start | bytes 1572872 | tf_op jit(solution)/shard_map/ppermute | solution.py:56
  262.1 44.9 %copy-start.20 = (bf16[256,4,2,128]{0,3,1,2:T(8,128)(2,1)S(1)}, bf16[256,4,2,128]{0,3,1,2:T(8,128)(2,1)}, u32[]{:S(2)}) copy-start(bf16[256,4,2,128]{0,3,1,2:T(8,128)(2,1)} %copy-done.19) | copy-start | bytes 1572868
  262.1 45.8 %copy-start.18 = (bf16[256,4,2,128]{0,3,1,2:T(8,128)(2,1)S(1)}, bf16[256,4,2,128]{0,3,1,2:T(8,128)(2,1)}, u32[]{:S(2)}) copy-start(bf16[256,4,2,128]{0,3,1,2:T(8,128)(2,1)} %copy-done.17) | copy-start | bytes 1572868
  262.1 46.7 %copy-start.16 = (bf16[256,4,2,128]{0,3,1,2:T(8,128)(2,1)S(1)}, bf16[256,4,2,128]{0,3,1,2:T(8,128)(2,1)}, u32[]{:S(2)}) copy-start(bf16[256,4,2,128]{0,3,1,2:T(8,128)(2,1)} %copy-done.15) | copy-start | bytes 1572868
  262.1 47.6 %copy-start.14 = (bf16[256,4,2,128]{0,3,1,2:T(8,128)(2,1)S(1)}, bf16[256,4,2,128]{0,3,1,2:T(8,128)(2,1)}, u32[]{:S(2)}) copy-start(bf16[256,4,2,128]{0,3,1,2:T(8,128)(2,1)} %copy-done.13) | copy-start | bytes 1572868
  262.1 48.5 %copy-start.12 = (bf16[256,4,2,128]{0,3,1,2:T(8,128)(2,1)S(1)}, bf16[256,4,2,128]{0,3,1,2:T(8,128)(2,1)}, u32[]{:S(2)}) copy-start(bf16[256,4,2,128]{0,3,1,2:T(8,128)(2,1)} %copy-done.11) | copy-start | bytes 1572868
  262.1 49.3 %copy-start.10 = (bf16[256,4,2,128]{0,3,1,2:T(8,128)(2,1)S(1)}, bf16[256,4,2,128]{0,3,1,2:T(8,128)(2,1)}, u32[]{:S(2)}) copy-start(bf16[256,4,2,128]{0,3,1,2:T(8,128)(2,1)} %copy-done.9) | copy-start | bytes 1572868
  262.1 50.2 %copy-start.8 = (bf16[256,4,2,128]{0,3,1,2:T(8,128)(2,1)S(1)}, bf16[256,4,2,128]{0,3,1,2:T(8,128)(2,1)}, u32[]{:S(2)}) copy-start(bf16[256,4,2,128]{0,3,1,2:T(8,128)(2,1)} %copy-done.7) | copy-start | bytes 1572868
  263.2 13.1 %collective-permute-start.14 = (bf16[256,4,2,128]{0,3,1,2:T(8,128)(2,1)}, bf16[256,4,2,128]{0,3,1,2:T(8,128)(2,1)S(1)}, u32[]{:S(2)}, u32[]{:S(2)}) collective-permute-start(bf16[256,4,2,128]{0,3,1,2:T(8,128)(2,1)} %collective-permute-done.13), channel_id=1, source_target_pairs={{0,2},{2,4},{4,6},{6,8},{8,10},{10,12},{12,14},{14,16},{16,18},{18... | collective-permute-start | bytes 1572872 | tf_op jit(solution)/shard_map/ppermute | solution.py:56
  334.1 10.0 %copy-start.2 = (bf16[128,4,4,128]{3,0,2,1:T(8,128)(2,1)S(1)}, bf16[128,4,4,128]{3,0,2,1:T(8,128)(2,1)}, u32[]{:S(2)}) copy-start(bf16[128,4,4,128]{3,0,2,1:T(8,128)(2,1)} %get-tuple-element.463) | copy-start | bytes 1572868 | tf_op jit(solution)/shard_map/while
  334.1 4.8 %copy-start.5 = (f32[4,4,128,128]{3,2,1,0:T(8,128)S(1)}, f32[4,4,128,128]{3,2,1,0:T(8,128)}, u32[]{:S(2)}) copy-start(f32[4,4,128,128]{3,2,1,0:T(8,128)} %get-tuple-element.127) | copy-start | bytes 3145732 | tf_op jit(solution)/shard_map/while/body/eval_jaxpr/cond
  341.8 1.0 copy-start.6
  344.0 3.6 copy-start.3
  350.6 1.0 copy-start.4
  358.0 10.0 %copy-start.2 = (bf16[128,4,4,128]{3,0,2,1:T(8,128)(2,1)S(1)}, bf16[128,4,4,128]{3,0,2,1:T(8,128)(2,1)}, u32[]{:S(2)}) copy-start(bf16[128,4,4,128]{3,0,2,1:T(8,128)(2,1)} %get-tuple-element.463) | copy-start | bytes 1572868 | tf_op jit(solution)/shard_map/while
  358.0 4.8 %copy-start.5 = (f32[4,4,128,128]{3,2,1,0:T(8,128)S(1)}, f32[4,4,128,128]{3,2,1,0:T(8,128)}, u32[]{:S(2)}) copy-start(f32[4,4,128,128]{3,2,1,0:T(8,128)} %get-tuple-element.127) | copy-start | bytes 3145732 | tf_op jit(solution)/shard_map/while/body/eval_jaxpr/cond
  365.7 1.0 copy-start.6
  367.9 3.6 copy-start.3
  374.5 1.0 copy-start.4
  381.9 10.0 %copy-start.2 = (bf16[128,4,4,128]{3,0,2,1:T(8,128)(2,1)S(1)}, bf16[128,4,4,128]{3,0,2,1:T(8,128)(2,1)}, u32[]{:S(2)}) copy-start(bf16[128,4,4,128]{3,0,2,1:T(8,128)(2,1)} %get-tuple-element.463) | copy-start | bytes 1572868 | tf_op jit(solution)/shard_map/while
  381.9 4.8 %copy-start.5 = (f32[4,4,128,128]{3,2,1,0:T(8,128)S(1)}, f32[4,4,128,128]{3,2,1,0:T(8,128)}, u32[]{:S(2)}) copy-start(f32[4,4,128,128]{3,2,1,0:T(8,128)} %get-tuple-element.127) | copy-start | bytes 3145732 | tf_op jit(solution)/shard_map/while/body/eval_jaxpr/cond
  389.6 1.0 copy-start.6
  391.9 3.6 copy-start.3
  398.4 1.0 copy-start.4
  405.8 10.0 %copy-start.2 = (bf16[128,4,4,128]{3,0,2,1:T(8,128)(2,1)S(1)}, bf16[128,4,4,128]{3,0,2,1:T(8,128)(2,1)}, u32[]{:S(2)}) copy-start(bf16[128,4,4,128]{3,0,2,1:T(8,128)(2,1)} %get-tuple-element.463) | copy-start | bytes 1572868 | tf_op jit(solution)/shard_map/while
  405.8 4.8 %copy-start.5 = (f32[4,4,128,128]{3,2,1,0:T(8,128)S(1)}, f32[4,4,128,128]{3,2,1,0:T(8,128)}, u32[]{:S(2)}) copy-start(f32[4,4,128,128]{3,2,1,0:T(8,128)} %get-tuple-element.127) | copy-start | bytes 3145732 | tf_op jit(solution)/shard_map/while/body/eval_jaxpr/cond
  413.5 1.0 copy-start.6
  415.8 3.6 copy-start.3
  422.3 1.0 copy-start.4
  423.3 4.6 %copy-start.1 = (bf16[256,4096]{1,0:T(8,128)(2,1)S(1)}, bf16[256,4096]{1,0:T(8,128)(2,1)}, u32[]{:S(2)}) copy-start(bf16[256,4096]{1,0:T(8,128)(2,1)} %param.11) | copy-start | bytes 6291460
  (5 other events, 4.0 us)
